TPU v7x, 32 devices: a whole 2x2x4 slice. The times are simulated.
32 devices in a mesh: slab: 8 (over z, x), pencil: 4 (over y, core).
Axes of the slice: x: 2, y: 2, z: 4, core: 2. Of those that a mesh axis runs over, the one named last changes fastest.
Arguments:
- sample_tile: int32 [8192, 1], P(('slab', 'pencil')), may hold values from 0 to 31; in each aligned block of 256 rows (0 to 255, 256 to 511, ...) at most 16 rows name the same one
- sample_cell: int32 [3, 8192], P(None, ('slab', 'pencil')), may hold values from 0 to 511, as said below
- sample_frac: float32 [3, 8192], P(None, ('slab', 'pencil')), may hold values from 0 to 1
- sample_value: float32 [2, 8192], P(None, ('slab', 'pencil')), may hold values from -24 to 24
Outputs:
- volume: float32 [2, 64, 512, 512], P(None, None, 'slab', 'pencil')
Inputs may be any that keep to these rules, and one draw needn't show every extreme that they name: `sample_tile`: among the 256 samples of one device no tile is named more than 16 times, and that count is reached in some device's block. `sample_cell`: row 0 is below 8, row 1 below 128, row 2 below 512.
All inputs are finite; a program needn't handle non-finite values.
Results may differ from a plain program's by a relative error of at most 0.0003.
Values sent between devices are 32-bit elements; how exact they have to be, the bound alone decides.
A program may use at most 64 MiB of HBM per device.

v0:
```python
import math

import jax
import jax.numpy as jnp
from jax import lax
from jax.sharding import PartitionSpec as P

NY = 512
NX = 512
PLANES = 8


beta_shape = 18.64


def from_behind(block, axis, distance):
    devices = range(lax.axis_size(axis))
    route = [((i - distance) % len(devices), i) for i in devices]
    return lax.ppermute(block, axis, route)


def bessel_zero(value):
    quarter = value * value * 0.25
    term = jnp.ones_like(value)
    total = jnp.ones_like(value)
    for order in range(1, 41):
        term = term * quarter / float(order * order)
        total = total + term
    return total


def kernel_weights(offset):
    tap_offsets = jnp.arange(8, dtype=jnp.float32) - 3.0
    scaled_gap = (tap_offsets[None, :] - offset[:, None]) * 0.25
    radicand = jnp.maximum(1.0 - scaled_gap * scaled_gap, 0.0)
    numerator = bessel_zero(beta_shape * jnp.sqrt(radicand))
    return numerator / bessel_zero(jnp.full((), beta_shape, jnp.float32))


def dft_tables(length):
    counter = jnp.arange(length, dtype=jnp.int32)
    phase_index = counter[:, None] * counter[None, :] % length
    angles = phase_index.astype(jnp.float32) * jnp.float32(2.0 * math.pi / length)
    factor = jnp.float32(1.0 / math.sqrt(length))
    cosine = jnp.cos(angles) * factor
    sine = jnp.sin(angles) * factor
    return (cosine, sine, cosine + sine)


def placed_weights(tap_weight, anchor, length, wrap):
    positions = jnp.arange(length, dtype=jnp.int32)
    placed = jnp.zeros((anchor.shape[0], length), jnp.float32)
    for tap in range(8):
        where_at = anchor + tap
        if wrap:
            where_at = where_at % length
        hit = (positions[None, :] == where_at[:, None]).astype(jnp.float32)
        placed = placed + hit * tap_weight[:, tap][:, None]
    return placed


def spread_grid(cells, records, depth_cells, row_count):
    sample_count = cells.shape[1]
    height_cells = row_count + 7
    weight_z = kernel_weights(records[0])
    weight_y = kernel_weights(records[1])
    weight_x = kernel_weights(records[2])
    plane_table = placed_weights(weight_z, cells[0], depth_cells, False)
    row_table = placed_weights(weight_y, cells[1], height_cells, False)
    column_table = placed_weights(weight_x, cells[2], NX, True)
    left_table = (plane_table[:, :, None] * row_table[:, None, :]).reshape(
        sample_count, depth_cells * height_cells
    )
    real_right = column_table * records[3][:, None]
    imag_right = column_table * records[4][:, None]
    numbers = (((0,), (0,)), ((), ()))
    real_grid = lax.dot_general(
        left_table,
        real_right,
        numbers,
        precision=lax.Precision.HIGHEST,
        preferred_element_type=jnp.float32,
    )
    imag_grid = lax.dot_general(
        left_table,
        imag_right,
        numbers,
        precision=lax.Precision.HIGHEST,
        preferred_element_type=jnp.float32,
    )
    return jnp.stack([real_grid, imag_grid]).reshape(2, depth_cells, height_cells, NX)


def product(left, right):
    return jnp.dot(left, right, precision=lax.Precision.HIGHEST, preferred_element_type=jnp.float32)


def shards(sample_tile, sample_cell, sample_frac, sample_value):
    n_slab = lax.axis_size("slab")
    n_pencil = lax.axis_size("pencil")
    tile_count = n_slab * n_pencil
    sample_count = sample_tile.shape[0]
    capacity = max(2, 2 * sample_count // tile_count)
    row_count = NY // n_pencil
    planes = PLANES
    owner_tile = sample_tile[:, 0]
    sort_order = jnp.argsort(owner_tile, stable=True)
    sorted_owner = owner_tile[sort_order]
    tile_ids = jnp.arange(tile_count, dtype=jnp.int32)
    tile_loads = jnp.sum((sorted_owner[:, None] == tile_ids[None, :]).astype(jnp.int32), axis=0)
    starts = jnp.cumsum(tile_loads) - tile_loads
    sorted_rank = jnp.arange(sample_count, dtype=jnp.int32) - starts[sorted_owner]
    slot_rank = jnp.zeros((sample_count,), jnp.int32).at[sort_order].set(sorted_rank)
    records = jnp.concatenate([sample_frac, sample_value], axis=0)
    slot_count = 2 * capacity
    next_owner = (owner_tile // n_pencil + 1) % n_slab * n_pencil + owner_tile % n_pencil
    lowered = sample_cell.at[0].add(-planes)
    first_slot = owner_tile * slot_count + slot_rank
    second_slot = next_owner * slot_count + capacity + slot_rank
    cell_buffer = jnp.zeros((3, tile_count * slot_count), jnp.int32)
    cell_buffer = cell_buffer.at[:, first_slot].set(sample_cell).at[:, second_slot].set(lowered)
    record_buffer = jnp.zeros((5, tile_count * slot_count), jnp.float32)
    record_buffer = record_buffer.at[:, first_slot].set(records).at[:, second_slot].set(records)
    cell_buffer = cell_buffer.reshape(3, n_slab, n_pencil, slot_count)
    record_buffer = record_buffer.reshape(5, n_slab, n_pencil, slot_count)
    got_cells, got_records = (
        lax.all_to_all(
            lax.all_to_all(cell_buffer, "slab", split_axis=1, concat_axis=1, tiled=True),
            "pencil",
            split_axis=2,
            concat_axis=2,
            tiled=True,
        ),
        lax.all_to_all(
            lax.all_to_all(record_buffer, "slab", split_axis=1, concat_axis=1, tiled=True),
            "pencil",
            split_axis=2,
            concat_axis=2,
            tiled=True,
        ),
    )
    field_grid = spread_grid(
        got_cells.reshape(3, -1), got_records.reshape(5, -1), planes, row_count
    )
    row_rim = from_behind(field_grid[:, :, row_count:], "pencil", 1)
    field_grid = field_grid[:, :, :row_count].at[:, :, :7].add(row_rim)
    cos_x, sin_x, both_x = dft_tables(NX)
    flat_real = field_grid[0].reshape(planes * row_count, NX)
    flat_imag = field_grid[1].reshape(planes * row_count, NX)
    first_term = product(flat_real, cos_x)
    second_term = product(flat_imag, sin_x)
    third_term = product(flat_real + flat_imag, both_x)
    turned_real = (first_term - second_term).reshape(planes, row_count, NX)
    turned_imag = (third_term - first_term - second_term).reshape(planes, row_count, NX)
    cos_y, sin_y, both_y = dft_tables(NY)
    part_real = lax.all_to_all(turned_real, "pencil", split_axis=2, concat_axis=1, tiled=True)
    part_imag = lax.all_to_all(turned_imag, "pencil", split_axis=2, concat_axis=1, tiled=True)
    first_part = jnp.einsum(
        "nyx,ym->nmx",
        part_real,
        cos_y,
        precision=lax.Precision.HIGHEST,
        preferred_element_type=jnp.float32,
    )
    second_part = jnp.einsum(
        "nyx,ym->nmx",
        part_imag,
        sin_y,
        precision=lax.Precision.HIGHEST,
        preferred_element_type=jnp.float32,
    )
    third_part = jnp.einsum(
        "nyx,ym->nmx",
        part_real + part_imag,
        both_y,
        precision=lax.Precision.HIGHEST,
        preferred_element_type=jnp.float32,
    )
    middle_real = first_part - second_part
    middle_imag = third_part - first_part - second_part
    cos_z, sin_z, both_z = dft_tables(planes * n_slab)
    part_real = lax.all_to_all(middle_real, "slab", split_axis=1, concat_axis=0, tiled=True)
    part_imag = lax.all_to_all(middle_imag, "slab", split_axis=1, concat_axis=0, tiled=True)
    first_part = jnp.einsum(
        "zyx,zm->myx",
        part_real,
        cos_z,
        precision=lax.Precision.HIGHEST,
        preferred_element_type=jnp.float32,
    )
    second_part = jnp.einsum(
        "zyx,zm->myx",
        part_imag,
        sin_z,
        precision=lax.Precision.HIGHEST,
        preferred_element_type=jnp.float32,
    )
    third_part = jnp.einsum(
        "zyx,zm->myx",
        part_real + part_imag,
        both_z,
        precision=lax.Precision.HIGHEST,
        preferred_element_type=jnp.float32,
    )
    final_real = first_part - second_part
    final_imag = third_part - first_part - second_part
    return jnp.stack([final_real, final_imag])


def solution(mesh):
    placed = (
        P(("slab", "pencil"), None),
        P(None, ("slab", "pencil")),
        P(None, ("slab", "pencil")),
        P(None, ("slab", "pencil")),
    )
    return jax.shard_map(
        shards,
        mesh=mesh,
        in_specs=placed,
        out_specs=P(None, None, "slab", "pencil"),
        check_vma=False,
    )
```

profile of v0, /device:TPU:0, one launch (start us, length us, event | category | flops | bytes accessed | tf_op | source)
XLA Modules:
  0.0 354.3 jit_solution(5115085824813003113)
XLA Ops:
  0.7 3.8 %sort.17 = (s32[256]{0:T(256)}, s32[256]{0:T(256)S(1)}) sort(s32[256]{0:T(256)} %bitcast.174, s32[256]{0:T(256)S(1)} %iota.109), dimensions={0}, to_apply=%region_0.0 | sort | flops 2048 | bytes 4096 | tf_op jit(solution)/shard_map/jit(argsort)/sort | solution.py:107
  8.4 4.3 %compare_select_fusion.1 = (s32[256,1]{0,1:T(1,128)S(1)}, s32[256,1]{0,1:T(1,128)S(1)}) fusion(s32[]{:T(128)} %bitcast.30, s32[]{:T(128)} %bitcast.31, s32[]{:T(128)} %bitcast.32, s32[]{:T(128)} %bitcast.33, s32[]{:T(128)} %bitcast.34, s32[]{:T(128)} %bitcast.36, s32[]{:T(128)} %bitcast.35, s32[256,1]{0,1:T(1,128)S(1)} %bitcast.236), kind=kLoop, calls=%fused_computation.186 | loop fusion | flops 3840 | bytes 3100 | tf_op jit(solution)/shard_map/gather | solution.py:112
  12.9 15.7 %select_subtract_fusion = s32[256]{0:T(256)S(1)} fusion(pred[256]{0:T(512)(128)(4,1)S(1)} %get-tuple-element.55, pred[256]{0:T(512)(128)(4,1)S(1)} %get-tuple-element.54, pred[256]{0:T(512)(128)(4,1)S(1)} %get-tuple-element.53, pred[256]{0:T(512)(128)(4,1)S(1)} %get-tuple-element.52, pred[256]{0:T(512)(128)(4,1)S(1)} %get-tuple-element.51, ...), kind=kLoop, calls=%fused_computation.220 | loop fusion | flops 6656 | bytes 8548 | tf_op jit(solution)/shard_map/sub | solution.py:112
  34.7 7.3 %all-to-all-start = ((s32[8,1,384]{2,1,0:T(1,128)}), s32[8,1,384]{2,1,0:T(1,128)S(1)}, u32[]{:S(2)}, u32[]{:S(2)}) async-start(s32[8,1,384]{2,1,0:T(1,128)} %reshape.1138), calls=%async_computation | async-start | bytes 24576 | tf_op jit(solution)/shard_map/all_to_all | solution.py:128
  42.0 6.5 %all-to-all-done = s32[8,1,384]{2,1,0:T(1,128)S(1)} async-done(((s32[8,1,384]{2,1,0:T(1,128)}), s32[8,1,384]{2,1,0:T(1,128)S(1)}, u32[]{:S(2)}, u32[]{:S(2)}) %all-to-all-start) | async-done | bytes 12320 | tf_op jit(solution)/shard_map/all_to_all | solution.py:128
  61.8 5.5 %all-to-all-done.2 = f32[8,1,640]{2,1,0:T(1,128)S(1)} async-done(((f32[8,1,640]{2,1,0:T(1,128)}), f32[8,1,640]{2,1,0:T(1,128)S(1)}, u32[]{:S(2)}, u32[]{:S(2)}) %all-to-all-start.2) | async-done | bytes 20512 | tf_op jit(solution)/shard_map/all_to_all | solution.py:135
  81.7 4.9 %mul.941 = f32[1024,1080]{0,1:T(8,128)} reshape(f32[1024,8,135]{0,2,1:T(8,128)} %broadcast_multiply_fusion) | data formatting | bytes 8847360 | tf_op jit(solution)/shard_map/mul | solution.py:71
  86.6 4.8 %reshape.921 = f32[8,135,1024]{2,1,0:T(8,128)} reshape(f32[1080,1024]{1,0:T(8,128)} %bitcast.183) | data formatting | bytes 8847360 | tf_op jit(solution)/shard_map/reshape.869
  91.4 11.9 %fusion.25 = f32[1,8,135,512]{3,2,1,0:T(8,128)S(1)} fusion(f32[8,135,1024]{2,1,0:T(8,128)} %reshape.921, f32[1024]{0:T(1024)S(1)} %mul.1013, f32[1024]{0:T(1024)S(1)} %bitcast.222, s32[1024]{0:T(1024)S(1)} %get-tuple-element.99, f32[1024]{0:T(1024)S(1)} %bitcast.224, s32[1024]{0:T(1024)S(1)} %get-tuple-element.98, f32[1024]{0:T(1024)S(1)} %bitcast.226, ...), kind=kOutput, calls=%fused_computation.50 | convolution fusion | flops 6807355392 | bytes 6705152 | tf_op jit(solution)/shard_map/dot_general | solution.py:84
  103.3 9.7 %fusion.22 = f32[1,8,135,512]{3,2,1,0:T(8,128)S(1)} fusion(f32[8,135,1024]{2,1,0:T(8,128)S(1)} %copy-done.5, f32[1024]{0:T(1024)S(1)} %mul.1010, f32[1024]{0:T(1024)S(1)} %bitcast.223, s32[1024]{0:T(1024)S(1)} %get-tuple-element.99, f32[1024]{0:T(1024)S(1)} %bitcast.225, s32[1024]{0:T(1024)S(1)} %get-tuple-element.98, f32[1024]{0:T(1024)S(1)} %bitcast.227, ...), kind=kOutput, calls=%fused_computation.49 | convolution fusion | flops 6807355392 | bytes 6705152 | tf_op jit(solution)/shard_map/dot_general | solution.py:77
  123.8 8.4 %fusion.47 = f32[1024,512]{1,0:T(8,128)S(1)} fusion(f32[1024,512]{1,0:T(8,128)S(1)} %bitcast.188), kind=kOutput, calls=%fused_computation.71 | convolution fusion | flops 3225157632 | bytes 4194304 | tf_op jit(solution)/shard_map/dot_general | solution.py:95
  132.3 8.8 %fusion.152 = (f32[1024,512]{1,0:T(8,128)}, f32[1024,512]{1,0:T(8,128)S(1)}) fusion(f32[1024,512]{1,0:T(8,128)S(1)} %fusion.47, f32[1024,512]{1,0:T(8,128)S(1)} %bitcast.181), kind=kOutput, calls=%fused_computation.280 | convolution fusion | flops 3225681920 | bytes 8388608 | tf_op jit(solution)/shard_map/dot_general | solution.py:95
  141.0 7.9 %subtract_subtract_fusion = f32[1024,512]{1,0:T(8,128)S(1)} fusion(f32[1024,512]{1,0:T(8,128)S(1)} %fusion.47, f32[1024,512]{1,0:T(8,128)S(1)} %get-tuple-element.152, f32[1024,512]{1,0:T(8,128)S(1)} %bitcast.182, f32[1024,512]{1,0:T(8,128)S(1)} %bitcast.189), kind=kOutput, calls=%fused_computation.31 | convolution fusion | flops 3227254784 | bytes 10485760 | tf_op jit(solution)/shard_map/dot_general | solution.py:95
  157.4 22.7 %all-to-all-done.5 = f32[8,128,512]{1,0,2:T(8,128)S(1)} async-done(((f32[8,128,512]{1,0,2:T(8,128)}), f32[8,128,512]{1,0,2:T(8,128)S(1)}, u32[]{:S(2)}, u32[]{:S(2)}) %all-to-all-start.5) | async-done | bytes 2097184 | tf_op jit(solution)/shard_map/all_to_all | solution.py:157
  181.4 4.6 %all-to-all-start.4 = ((f32[8,128,512]{1,0,2:T(8,128)}), f32[8,128,512]{1,0,2:T(8,128)}, u32[]{:S(2)}, u32[]{:S(2)}) async-start(f32[8,128,512]{1,0,2:T(8,128)} %copy.70), calls=%async_computation.4 | async-start | bytes 4194304 | tf_op jit(solution)/shard_map/all_to_all | solution.py:156
  188.0 23.8 %all-to-all-done.4 = f32[8,128,512]{1,0,2:T(8,128)} async-done(((f32[8,128,512]{1,0,2:T(8,128)}), f32[8,128,512]{1,0,2:T(8,128)}, u32[]{:S(2)}, u32[]{:S(2)}) %all-to-all-start.4) | async-done | bytes 2097184 | tf_op jit(solution)/shard_map/all_to_all | solution.py:156
  214.7 9.0 %fusion.38 = f32[512,8,128]{2,0,1:T(8,128)S(1)} fusion(f32[8,512,128]{2,1,0:T(8,128)} %bitcast.184), kind=kOutput, calls=%fused_computation.60 | convolution fusion | flops 3225157632 | bytes 4194304 | tf_op jit(solution)/shard_map/nyx,ym->nmx/dot_general | solution.py:158
  223.6 9.2 %bitcast_subtract_fusion.1 = (f32[8,512,128]{2,1,0:T(8,128)S(1)}, f32[512,8,128]{2,0,1:T(8,128)}) fusion(f32[512,8,128]{2,0,1:T(8,128)S(1)} %fusion.38, f32[8,512,128]{2,1,0:T(8,128)S(1)} %bitcast.179), kind=kOutput, calls=%fused_computation.22 | convolution fusion | flops 3225681920 | bytes 8388608 | tf_op jit(solution)/shard_map/nyx,ym->nmx/dot_general | solution.py:165
  239.0 11.1 %fusion.7 = f32[8,512,128]{2,1,0:T(8,128)S(1)} fusion(f32[512,8,128]{2,0,1:T(8,128)} %get-tuple-element.154, f32[512,8,128]{2,0,1:T(8,128)} %copy-done.4, f32[8,512,128]{2,1,0:T(8,128)} %bitcast.185, f32[8,512,128]{2,1,0:T(8,128)} %bitcast.180), kind=kOutput, calls=%fused_computation.21 | convolution fusion | flops 3227254784 | bytes 10485760 | tf_op jit(solution)/shard_map/nyx,ym->nmx/dot_general | solution.py:172
  252.7 34.4 %all-to-all-done.6 = f32[8,512,128]{2,0,1:T(8,128)S(1)} async-done(((f32[8,512,128]{2,0,1:T(8,128)}), f32[8,512,128]{2,0,1:T(8,128)S(1)}, u32[]{:S(2)}, u32[]{:S(2)}) %all-to-all-start.6) | async-done | bytes 2097184 | tf_op jit(solution)/shard_map/all_to_all | solution.py:182
  288.4 4.6 %all-to-all-start.7 = ((f32[8,512,128]{2,0,1:T(8,128)}), f32[8,512,128]{2,0,1:T(8,128)}, u32[]{:S(2)}, u32[]{:S(2)}) async-start(f32[8,512,128]{2,0,1:T(8,128)} %copy.76), calls=%async_computation.7 | async-start | bytes 4194304 | tf_op jit(solution)/shard_map/all_to_all | solution.py:183
  296.6 44.2 %all-to-all-done.7 = f32[8,512,128]{2,0,1:T(8,128)} async-done(((f32[8,512,128]{2,0,1:T(8,128)}), f32[8,512,128]{2,0,1:T(8,128)}, u32[]{:S(2)}, u32[]{:S(2)}) %all-to-all-start.7) | async-done | bytes 2097184 | tf_op jit(solution)/shard_map/all_to_all | solution.py:183
  344.6 3.9 %subtract_bitcast_fusion = f32[1,64,64,128]{3,1,2,0:T(8,128)S(1)} fusion(f32[64,64,128]{2,0,1:T(8,128)S(1)} %fusion.1, f32[64,64,128]{2,0,1:T(8,128)S(1)} %fusion.5, f32[8,8,64,128]{3,0,2,1:T(8,128)} %bitcast.93, f32[8,8,64,128]{3,0,2,1:T(8,128)S(1)} %bitcast.178), kind=kOutput, calls=%fused_computation.27 | convolution fusion | flops 404295680 | bytes 10485760 | tf_op jit(solution)/shard_map/zyx,zm->myx/dot_general | solution.py:198
  349.5 4.4 %copy.78 = f32[2,64,64,128]{3,2,1,0:T(8,128)} copy(f32[2,64,64,128]{3,1,2,0:T(8,128)S(1)} %pad_maximum_fusion) | data formatting | bytes 8388608 | tf_op jit(solution)/shard_map/stack | solution.py:207
  (111 shorter events, 81.8 us)
Async XLA Ops:
  0.0 42.0 %copy-start.6 = (f32[3,256]{1,0:T(4,128)S(1)}, f32[3,256]{1,0:T(4,128)}, u32[]{:S(2)}) copy-start(f32[3,256]{1,0:T(4,128)} %param.10) | copy-start | bytes 9220
  0.0 42.0 %copy-start.7 = (f32[2,256]{1,0:T(2,128)S(1)}, f32[2,256]{1,0:T(2,128)}, u32[]{:S(2)}) copy-start(f32[2,256]{1,0:T(2,128)} %param.11) | copy-start | bytes 6148
  34.7 13.8 %all-to-all-start = ((s32[8,1,384]{2,1,0:T(1,128)}), s32[8,1,384]{2,1,0:T(1,128)S(1)}, u32[]{:S(2)}, u32[]{:S(2)}) async-start(s32[8,1,384]{2,1,0:T(1,128)} %reshape.1138), calls=%async_computation | async-start | bytes 24576 | tf_op jit(solution)/shard_map/all_to_all | solution.py:128
  50.4 7.1 %all-to-all-start.1 = ((s32[4,1,768]{2,1,0:T(1,128)}), s32[4,1,768]{2,1,0:T(1,128)S(1)}, u32[]{:S(2)}, u32[]{:S(2)}) async-start(s32[4,1,768]{2,1,0:T(1,128)} %reshape.1140), calls=%async_computation.1 | async-start | bytes 24576 | tf_op jit(solution)/shard_map/all_to_all | solution.py:127
  57.5 9.9 %all-to-all-start.2 = ((f32[8,1,640]{2,1,0:T(1,128)}), f32[8,1,640]{2,1,0:T(1,128)S(1)}, u32[]{:S(2)}, u32[]{:S(2)}) async-start(f32[8,1,640]{2,1,0:T(1,128)} %reshape.1134), calls=%async_computation.2 | async-start | bytes 40960 | tf_op jit(solution)/shard_map/all_to_all | solution.py:135
  69.5 7.1 %all-to-all-start.3 = ((f32[4,1,1280]{2,1,0:T(1,128)}), f32[4,1,1280]{2,1,0:T(1,128)S(1)}, u32[]{:S(2)}, u32[]{:S(2)}) async-start(f32[4,1,1280]{2,1,0:T(1,128)} %reshape.1136), calls=%async_computation.3 | async-start | bytes 40960 | tf_op jit(solution)/shard_map/all_to_all | solution.py:134
  91.4 11.9 %copy-start.5 = (f32[8,135,1024]{2,1,0:T(8,128)S(1)}, f32[8,135,1024]{2,1,0:T(8,128)}, u32[]{:S(2)}) copy-start(f32[8,135,1024]{2,1,0:T(8,128)} %reshape.921) | copy-start | bytes 13271044
  113.0 5.8 %collective-permute-start = (f32[2,8,7,512]{3,2,1,0:T(8,128)S(1)}, f32[2,8,7,512]{3,2,1,0:T(8,128)S(1)}, u32[]{:S(2)}, u32[]{:S(2)}) collective-permute-start(f32[2,8,7,512]{3,2,1,0:T(8,128)S(1)} %pad_maximum_fusion.1), channel_id=1, source_target_pairs={{3,0},{0,1},{1,2},{2,3},{7,4},{4,5},{5,6},{6,7},{11,8},{8,9},{9,10... | collective-permute-start | bytes 688136 | tf_op jit(solution)/shard_map/ppermute | solution.py:19
  150.9 29.2 %all-to-all-start.5 = ((f32[8,128,512]{1,0,2:T(8,128)}), f32[8,128,512]{1,0,2:T(8,128)S(1)}, u32[]{:S(2)}, u32[]{:S(2)}) async-start(f32[8,128,512]{1,0,2:T(8,128)} %copy.72), calls=%async_computation.5 | async-start | bytes 4194304 | tf_op jit(solution)/shard_map/all_to_all | solution.py:157
  180.1 1.3 copy-start.3
  181.4 30.3 %all-to-all-start.4 = ((f32[8,128,512]{1,0,2:T(8,128)}), f32[8,128,512]{1,0,2:T(8,128)}, u32[]{:S(2)}, u32[]{:S(2)}) async-start(f32[8,128,512]{1,0,2:T(8,128)} %copy.70), calls=%async_computation.4 | async-start | bytes 4194304 | tf_op jit(solution)/shard_map/all_to_all | solution.py:156
  188.0 35.6 %copy-start.2 = (f32[8,128,4,128]{3,1,2,0:T(8,128)}, f32[8,128,4,128]{3,1,2,0:T(8,128)S(1)}, u32[]{:S(2)}) copy-start(f32[8,128,4,128]{3,1,2,0:T(8,128)S(1)} %copy.73) | copy-start | bytes 6291460
  223.6 9.2 %copy-start.4 = (f32[512,8,128]{2,0,1:T(8,128)}, f32[512,8,128]{2,0,1:T(8,128)S(1)}, u32[]{:S(2)}) copy-start(f32[512,8,128]{2,0,1:T(8,128)S(1)} %fusion.38) | copy-start | bytes 6291460
  235.4 51.7 %all-to-all-start.6 = ((f32[8,512,128]{2,0,1:T(8,128)}), f32[8,512,128]{2,0,1:T(8,128)S(1)}, u32[]{:S(2)}, u32[]{:S(2)}) async-start(f32[8,512,128]{2,0,1:T(8,128)} %copy.74), calls=%async_computation.6 | async-start | bytes 4194304 | tf_op jit(solution)/shard_map/all_to_all | solution.py:182
  287.2 1.3 copy-start
  288.4 52.4 %all-to-all-start.7 = ((f32[8,512,128]{2,0,1:T(8,128)}), f32[8,512,128]{2,0,1:T(8,128)}, u32[]{:S(2)}, u32[]{:S(2)}) async-start(f32[8,512,128]{2,0,1:T(8,128)} %copy.76), calls=%async_computation.7 | async-start | bytes 4194304 | tf_op jit(solution)/shard_map/all_to_all | solution.py:183
  340.9 3.8 %copy-start.1 = (f32[8,512,128]{2,0,1:T(8,128)S(1)}, f32[8,512,128]{2,0,1:T(8,128)}, u32[]{:S(2)}) copy-start(f32[8,512,128]{2,0,1:T(8,128)} %copy-done) | copy-start | bytes 6291460
where the time goes:
time: 361 us; the launch traced here: 354 us
  waiting for transfers between devices  144 us (40%)
  matrix products  87.2 us (24%)
  local copies, waits for them, and re-layouts  53.4 us (15%)
  other arithmetic  34.9 us (10%)
  starting transfers between devices  34.1 us (9%)
    all_to_all x1, waiting for transfers between devices, shards(): lax.all_to_all(middle_imag, 'slab', split_axis=1, concat_axis=0, tiled=True)  44.2 us
    all_to_all x1, waiting for transfers between devices, shards(): lax.all_to_all(middle_real, 'slab', split_axis=1, concat_axis=0, tiled=True)  34.4 us
    dot_general x3, matrix products, product(): jnp.dot(left, right, precision=lax.Precision.HIGHEST, preferred_element_t...  25.1 us
    all_to_all x1, waiting for transfers between devices, shards(): lax.all_to_all(turned_real, 'pencil', split_axis=2, concat_axis=1, tiled=...  23.8 us
    all_to_all x1, waiting for transfers between devices, shards(): lax.all_to_all(turned_imag, 'pencil', split_axis=2, concat_axis=1, tiled=...  22.7 us
    sub x1, other arithmetic, shards(): jnp.arange(sample_count, dtype=jnp.int32) - starts[sorted_owner]  15.7 us
    dot_general x1, matrix products, spread_grid(): lax.dot_general(left_table, imag_right, numbers, precision=lax.Precision....  11.9 us
    dot_general x1, matrix products, shards(): jnp.einsum('nyx,ym->nmx', part_real + part_imag, both_y, precision=lax.Pr...  11.1 us
  transfers between devices with their start and end apart: 9, of which 8 were waited for; matrix products, arithmetic and copies ran while one was open for 8% of the time, Pallas kernels for 0%

commit v1 on v0

v1 whole, which is shorter than its diff:
```python
import functools
import math

import jax
import jax.numpy as jnp
import numpy as np
from jax import lax
from jax.experimental import pallas as pl
from jax.experimental.pallas import tpu as pltpu
from jax.sharding import PartitionSpec as P

NY = 512
NX = 512
PLANES = 8
TAPS = 8
WINDOW = PLANES + TAPS - 1
LOW = 16
CHUNK = 128
BETA = 18.64
F32 = jnp.float32
BF16 = jnp.bfloat16


def series():
    quarter = BETA * BETA / 4.0
    terms = [1.0]
    for order in range(1, 41):
        terms.append(terms[-1] * quarter / float(order * order))
    total = sum(terms)
    return [term / total for term in terms]


SERIES = series()


def tap_weights(frac, taps):
    gap = (taps - 3.0 - frac) * 0.25
    radicand = jnp.maximum(1.0 - gap * gap, 0.0)
    total = jnp.full(radicand.shape, SERIES[-1], F32)
    for coefficient in SERIES[-2::-1]:
        total = total * radicand + coefficient
    return total


def placed(weights, anchor, rows):
    gap = lax.broadcasted_iota(jnp.int32, (rows, anchor.shape[1]), 0) - anchor
    total = jnp.where(gap == 0, weights[0:1], 0.0)
    for tap in range(1, TAPS):
        total = jnp.where(gap == tap, weights[tap : tap + 1], total)
    return total


def halves(value):
    high = value.astype(BF16)
    return high, (value - high.astype(F32)).astype(BF16)


def fine_dot(left, right):
    left_high, left_low = left
    right_high, right_low = halves(right)
    dot = functools.partial(jnp.dot, preferred_element_type=F32)
    return dot(left_high, right_high) + (dot(left_high, right_low) + dot(left_low, right_high))


def kernel(
    n_src, n_slab, per, room, ny, nz,
    starts, feats, tap_y, phase_y, tap_x, phase_x, table_z, out, rows, packed, grid_re, grid_im, left,
):
    slab_here = lax.axis_index("slab")
    pencil_here = lax.axis_index("pencil")
    nx = out.shape[2]

    @pl.loop(0, n_src)
    def _(src):
        rows[pl.ds(pl.multiple_of(src * per, per), per), 0:8] = feats[src].T

    grid_re[...] = jnp.zeros_like(grid_re)
    grid_im[...] = jnp.zeros_like(grid_im)
    taps = lax.broadcasted_iota(jnp.int32, (TAPS, CHUNK), 0).astype(F32)
    lanes = lax.broadcasted_iota(jnp.int32, (8, CHUNK), 1)
    ty, hy = halves(tap_y[slab_here]), halves(phase_y[slab_here])
    tx, hx = halves(tap_x[pencil_here]), halves(phase_x[pencil_here])

    @pl.loop(0, n_slab)
    def _(slab):
        def pack(src, filled):
            first = starts[src, slab]
            packed[pl.ds(filled, room), :] = rows[pl.ds(src * per + first, room), :]
            return filled + starts[src, slab + 1] - first

        filled = lax.fori_loop(0, n_src, pack, jnp.int32(0))

        @pl.loop(0, (filled + CHUNK - 1) // CHUNK)
        def _(chunk):
            base = pl.multiple_of(chunk * CHUNK, CHUNK)
            f = packed[pl.ds(base, CHUNK), :].T[0:8]
            f = jnp.where(lanes + base < filled, f, 0.0)
            whole = f[0:3].astype(jnp.int32)
            depth = whole[0:1] - slab * PLANES
            high_y, high_x = whole[1:2] // LOW, whole[2:3] // LOW
            low_y, low_x = whole[1:2] - high_y * LOW, whole[2:3] - high_x * LOW
            weight_z = placed(tap_weights(f[3:4], taps), depth, 2 * PLANES)
            place_y = placed(tap_weights(f[4:5], taps), low_y, 2 * LOW)
            place_x = placed(tap_weights(f[5:6], taps), low_x, 2 * LOW)
            counter = lax.broadcasted_iota(jnp.int32, (NY // LOW, CHUNK), 0)
            hit_y = counter == high_y
            hit_x = (counter == high_x).astype(F32)
            value_y = jnp.concatenate([jnp.where(hit_y, f[6:7], 0.0), jnp.where(hit_y, f[7:8], 0.0)], axis=0)
            near, far = fine_dot(ty, place_y), fine_dot(hy, value_y)
            b_re = near[:ny] * far[:ny] - near[ny:] * far[ny:]
            b_im = near[:ny] * far[ny:] + near[ny:] * far[:ny]
            near, far = fine_dot(tx, place_x), fine_dot(hx, hit_x)
            c_re = near[:nx] * far[:nx] - near[nx:] * far[nx:]
            c_im = near[:nx] * far[nx:] + near[nx:] * far[:nx]
            right = jnp.concatenate(
                [jnp.concatenate([c_re, -c_im], axis=1), jnp.concatenate([c_im, c_re], axis=1)], axis=0
            )
            right_high, right_low = halves(right)
            both = jnp.concatenate([b_re, b_im], axis=1)
            for z in range(WINDOW):
                line = weight_z[z : z + 1]
                high, low = halves(both * jnp.concatenate([line, line], axis=1))
                left[z * ny : (z + 1) * ny, 0 : 2 * CHUNK] = high
                left[z * ny : (z + 1) * ny, 2 * CHUNK : 4 * CHUNK] = low
                left[z * ny : (z + 1) * ny, 4 * CHUNK : 6 * CHUNK] = high
            right_all = jnp.concatenate([right_high, right_high, right_low], axis=1)
            sums = lax.dot_general(
                left[...], right_all, (((1,), (1,)), ((), ())), preferred_element_type=F32
            )
            at = pl.ds(pl.multiple_of(slab * (PLANES * ny), PLANES * ny), WINDOW * ny)
            grid_re[at, :] += sums[:, :nx]
            grid_im[at, :] += sums[:, nx:]

    depth_all = table_z.shape[1]
    tz = halves(table_z[...])

    @pl.loop(0, ny)
    def _(row):
        pick = pl.ds(row, depth_all, stride=ny)
        sums = fine_dot(tz, jnp.concatenate([grid_re[pick, :], grid_im[pick, :]], axis=1))
        place = pl.ds(row, nz, stride=ny)
        out[0, place, :] = sums[:nz, :nx] - sums[nz:, nx:]
        out[1, place, :] = sums[nz:, :nx] + sums[:nz, nx:]


def turns(outer, inner, length):
    angle = 2.0 * np.pi * ((outer * inner) % length) / length
    return np.cos(angle), np.sin(angle)


def tables(n_slab, n_pencil, nz):
    ny, nx = NY // n_slab, NX // n_pencil
    near, far = np.arange(2 * LOW), np.arange(NY // LOW) * LOW

    def stacked(count, width, inner, length):
        outer = np.arange(count * width).reshape(count, width, 1)
        return turns(outer, inner, length)

    cy, sy = stacked(n_slab, ny, near, NY)
    tap_y = np.concatenate([cy, sy], axis=1)
    cy, sy = stacked(n_slab, ny, far, NY)
    phase_y = np.concatenate(
        [np.concatenate([cy, -sy], axis=2), np.concatenate([sy, cy], axis=2)], axis=1
    )
    cx, sx = stacked(n_pencil, nx, near, NX)
    tap_x = np.concatenate([cx, sx], axis=1)
    cx, sx = stacked(n_pencil, nx, far, NX)
    phase_x = np.concatenate([cx, sx], axis=1)
    cz, sz = turns(np.arange(nz)[:, None], np.arange(nz + PLANES)[None, :], nz)
    table_z = np.concatenate([cz, sz], axis=0) / math.sqrt(nz * NY * NX)
    return [x.astype(np.float32) for x in (tap_y, phase_y, tap_x, phase_x, table_z)]


def shards(n_slab, n_pencil, sample_tile, sample_cell, sample_frac, sample_value):
    n_src = n_slab * n_pencil
    per = sample_tile.shape[0]
    nz = PLANES * n_slab
    ny, nx = NY // n_slab, NX // n_pencil
    capacity = max(2, 2 * per // n_src)
    room = -(-n_pencil * capacity // 8) * 8
    owner = sample_tile[:, 0]
    base_z = owner // n_pencil * PLANES + sample_cell[0]
    base_y = owner % n_pencil * (NY // n_pencil) + sample_cell[1]
    anchor = jnp.stack([base_z, base_y, sample_cell[2]]).astype(F32)
    mine = jnp.concatenate([anchor, sample_frac, sample_value], axis=0)
    order = jnp.arange(per, dtype=jnp.int32)
    key = base_z * per + order
    rank = jnp.sum((key[None, :] < key[:, None]).astype(jnp.int32), axis=1)
    shuffle = (rank[:, None] == order[None, :]).astype(F32)
    mine = jnp.dot(mine, shuffle, precision=lax.Precision.HIGHEST, preferred_element_type=F32)
    feats = lax.all_gather(mine, ("slab", "pencil"), axis=0, tiled=False)
    slab_of = feats[:, 0, :].astype(jnp.int32) // PLANES
    bins = jnp.arange(n_slab + 1, dtype=jnp.int32)
    starts = jnp.sum((slab_of[:, None, :] < bins[None, :, None]).astype(jnp.int32), axis=2)
    most = n_src * room
    vmem = pl.BlockSpec(memory_space=pltpu.VMEM)
    volume = pl.pallas_call(
        functools.partial(kernel, n_src, n_slab, per, room, ny, nz),
        out_shape=jax.ShapeDtypeStruct((2, nz * ny, nx), F32),
        in_specs=[pl.BlockSpec(memory_space=pltpu.SMEM)] + [vmem] * 6,
        out_specs=vmem,
        scratch_shapes=[
            pltpu.VMEM((n_src * per + room, 128), F32),
            pltpu.VMEM((most + room, 128), F32),
            pltpu.VMEM(((nz + PLANES) * ny, nx), F32),
            pltpu.VMEM(((nz + PLANES) * ny, nx), F32),
            pltpu.VMEM((WINDOW * ny, 6 * CHUNK), BF16),
        ],
        compiler_params=pltpu.CompilerParams(vmem_limit_bytes=62 * 1024 * 1024),
        name="volume",
    )(starts, feats, *tables(n_slab, n_pencil, nz))
    return volume.reshape(2, nz, ny, nx)


def solution(mesh):
    placed_as = (
        P(("slab", "pencil"), None),
        P(None, ("slab", "pencil")),
        P(None, ("slab", "pencil")),
        P(None, ("slab", "pencil")),
    )
    return jax.shard_map(
        functools.partial(shards, mesh.shape["slab"], mesh.shape["pencil"]),
        mesh=mesh,
        in_specs=placed_as,
        out_specs=P(None, None, "slab", "pencil"),
        check_vma=False,
    )
```

time: 361 us -> 150 us (0.42); the launches traced: 354 us -> 148 us
  waiting for transfers between devices: 144 us -> 0 us
  Pallas kernels: 0 us -> 101 us
  matrix products: 87.2 us -> 0.92 us
  local copies, waits for them, and re-layouts: 53.4 us -> 0.7 us
  blocking collectives: 0 us -> 44 us
  starting transfers between devices: 34.1 us -> 0 us
  other arithmetic: 34.9 us -> 2.13 us
    all_to_all x8 -> x0, waiting for transfers between devices: 141 us -> none  [the longest x1 44.2 us: shards(): lax.all_to_all(middle_imag, 'slab', split_axis=1, concat_axis=0, tiled=True)]
    pallas_call x0 -> x1, Pallas kernels: none -> 101 us  [shards(): pl.pallas_call(functools.partial(kernel, n_src, n_slab, per, room, ny, nz...]
    dot_general x11 -> x1, matrix products: 87.2 us -> 0.92 us  [shards(): jnp.dot(mine, shuffle, precision=lax.Precision.HIGHEST, preferred_element...]
    all_gather x0 -> x1, blocking collectives: none -> 44 us  [shards(): feats = lax.all_gather(mine, ('slab', 'pencil'), axis=0, tiled=False)]
    all_to_all x8 -> x0, starting transfers between devices: 34.1 us -> none  [the longest x1 7.28 us: shards(): lax.all_to_all(cell_buffer, 'slab', split_axis=1, concat_axis=1, tiled=True)]
    sub x3 -> x0, other arithmetic: 15.7 us -> none  [the longest x1 15.7 us: shards(): jnp.arange(sample_count, dtype=jnp.int32) - starts[sorted_owner]]
    another operation x3 -> x0, local copies, waits for them, and re-layouts: 9.36 us -> none
    scatter x5 -> x0, local copies, waits for them, and re-layouts: 6.71 us -> none  [the longest x2 2.66 us: shards(): cell_buffer.at[:, first_slot].set(sample_cell).at[:, second_slot]]
  transfers between devices with their start and end apart: 9 -> 0, of which waited for: 8 -> 0; matrix products, arithmetic and copies ran while one was open for 8% -> 0% of each run, Pallas kernels for 0% -> 0%
where the time goes in v1:
time: 150 us; the launch traced here: 148 us
  Pallas kernels  101 us (67%)
  blocking collectives  44 us (29%)
  other arithmetic  2.13 us (1%)
    pallas_call x1, Pallas kernels, shards(): pl.pallas_call(functools.partial(kernel, n_src, n_slab, per, room, ny, nz...  101 us
    all_gather x1, blocking collectives, shards(): feats = lax.all_gather(mine, ('slab', 'pencil'), axis=0, tiled=False)  44 us

profile of v1, /device:TPU:0, one launch (start us, length us, event | category | flops | bytes accessed | tf_op | source)
XLA Modules:
  0.0 148.5 jit_solution(15898262182943818078)
XLA Ops:
  0.0 0.7 fusion.10
  0.7 0.8 iota_add_fusion
  1.5 0.2 convert_reduce_fusion.1
  1.7 0.9 fusion
  2.6 44.0 %all-gather = f32[256,256]{1,0:T(8,128)S(1)} all-gather(f32[8,256]{1,0:T(8,128)S(1)} %fusion), channel_id=2, replica_groups=mesh['slab'=8,'pencil'=4] {'slab','pencil'}, dimensions={0}, use_global_device_ids=true | all-gather | bytes 270336 | tf_op jit(solution)/shard_map/all_gather | solution.py:191
  46.6 0.0 copy-start
  46.6 0.2 and_select_fusion
  46.8 0.2 convert_reduce_fusion
  47.1 0.7 copy.10.starts
  47.8 0.0 copy-done
  47.8 100.7 %volume.1 = f32[2,4096,128]{2,1,0:T(8,128)} custom-call(s32[32,9]{1,0:T(8,128)} %copy.10.starts, f32[32,8,256]{2,1,0:T(8,128)} %bitcast.32, f32[8,128,32]{2,1,0:T(8,128)} %constant.57.clone.tap_y, f32[8,128,64]{2,1,0:T(8,128)} %constant.58.clone.phase_y, f32[4,256,32]{2,1,0:T(8,128)} %constant.59.clone.tap_x, f32[4,256,32]{2,1,0:T(8,128)} %constant.60.clone.phase_x, ...), custom_call_target="tpu_custom_call" | custom-call | tf_op jit(solution)/shard_map/volume/pallas_call | solution.py:197
  (2 shorter events, 0.0 us)
Async XLA Ops:
  46.6 1.1 copy-start

commit v2 on v1

--- a/solution.py
+++ b/solution.py
@@ -16,6 +16,7 @@
 WINDOW = PLANES + TAPS - 1
 LOW = 16
 CHUNK = 128
+GROUP = 256
 BETA = 18.64
 F32 = jnp.float32
 BF16 = jnp.bfloat16
@@ -55,31 +56,100 @@
     return high, (value - high.astype(F32)).astype(BF16)
 
 
+def stack_left(value):
+    high = value.astype(jnp.bfloat16)
+    low = (value - high.astype(np.float32)).astype(jnp.bfloat16)
+    return np.concatenate([high, high, low], axis=-1)
+
+
 def fine_dot(left, right):
-    left_high, left_low = left
-    right_high, right_low = halves(right)
-    dot = functools.partial(jnp.dot, preferred_element_type=F32)
-    return dot(left_high, right_high) + (dot(left_high, right_low) + dot(left_low, right_high))
+    high, low = halves(right)
+    return jnp.dot(left, jnp.concatenate([high, low, high], axis=0), preferred_element_type=F32)
+
+
+def gather_kernel(n_slab, n_pencil, mine, out, send_sem, recv_sem, own_sem):
+    count = n_slab * n_pencil
+    me = lax.axis_index("slab") * n_pencil + lax.axis_index("pencil")
+
+    def name(step):
+        target = lax.rem(me + step, count)
+        return {"slab": target // n_pencil, "pencil": lax.rem(target, n_pencil)}
+
+    own = pltpu.make_async_copy(mine, out.at[me], own_sem)
+    own.start()
+    barrier = pltpu.get_barrier_semaphore()
+
+    @pl.loop(1, count)
+    def _(step):
+        pl.semaphore_signal(barrier, inc=1, device_id=name(step), device_id_type=pl.DeviceIdType.MESH)
+
+    pl.semaphore_wait(barrier, count - 1)
+
+    def send(step, slot):
+        return pltpu.make_async_remote_copy(
+            src_ref=mine,
+            dst_ref=out.at[slot],
+            send_sem=send_sem.at[step - 1],
+            recv_sem=recv_sem.at[step - 1],
+            device_id=name(step),
+            device_id_type=pl.DeviceIdType.MESH,
+        )
+
+    @pl.loop(1, count)
+    def _(step):
+        send(step, me).start()
+
+    own.wait()
+
+    @pl.loop(1, count)
+    def _(step):
+        send(step, lax.rem(me + count - step, count)).wait_recv()
+
+    @pl.loop(1, count)
+    def _(step):
+        send(step, me).wait_send()
+
+
+def gather_all(n_slab, n_pencil, mine):
+    count = n_slab * n_pencil
+    vmem = pl.BlockSpec(memory_space=pltpu.VMEM)
+    return pl.pallas_call(
+        functools.partial(gather_kernel, n_slab, n_pencil),
+        out_shape=jax.ShapeDtypeStruct((count,) + mine.shape, mine.dtype),
+        in_specs=[vmem],
+        out_specs=vmem,
+        scratch_shapes=[
+            pltpu.SemaphoreType.DMA((count - 1,)),
+            pltpu.SemaphoreType.DMA((count - 1,)),
+            pltpu.SemaphoreType.DMA,
+        ],
+        compiler_params=pltpu.CompilerParams(collective_id=0, has_side_effects=True),
+        name="gather_samples",
+    )(mine)
 
 
 def kernel(
     n_src, n_slab, per, room, ny, nz,
-    starts, feats, tap_y, phase_y, tap_x, phase_x, table_z, out, rows, packed, grid_re, grid_im, left,
+    starts, feats, tap_y, phase_y, tap_x, phase_x, table_z, out,
+    rows, packed, grid_re, grid_im, left, both, right, depths,
 ):
     slab_here = lax.axis_index("slab")
     pencil_here = lax.axis_index("pencil")
     nx = out.shape[2]
-
-    @pl.loop(0, n_src)
+    taps = lax.broadcasted_iota(jnp.int32, (TAPS, per), 0).astype(F32)
+
+    @pl.loop(0, n_src, unroll=2)
     def _(src):
-        rows[pl.ds(pl.multiple_of(src * per, per), per), 0:8] = feats[src].T
+        f = feats[src]
+        pieces = [f] + [tap_weights(f[3 + d : 4 + d], taps) for d in range(3)]
+        rows[pl.ds(pl.multiple_of(src * per, per), per), 0:32] = jnp.concatenate(pieces, axis=0).T
 
     grid_re[...] = jnp.zeros_like(grid_re)
     grid_im[...] = jnp.zeros_like(grid_im)
-    taps = lax.broadcasted_iota(jnp.int32, (TAPS, CHUNK), 0).astype(F32)
-    lanes = lax.broadcasted_iota(jnp.int32, (8, CHUNK), 1)
-    ty, hy = halves(tap_y[slab_here]), halves(phase_y[slab_here])
-    tx, hx = halves(tap_x[pencil_here]), halves(phase_x[pencil_here])
+    lanes = lax.broadcasted_iota(jnp.int32, (32, GROUP), 1)
+    counter = lax.broadcasted_iota(jnp.int32, (NY // LOW, GROUP), 0)
+    ty, hy = tap_y[slab_here], phase_y[slab_here]
+    tx, hx = tap_x[pencil_here], phase_x[pencil_here]
 
     @pl.loop(0, n_slab)
     def _(slab):
@@ -88,53 +158,62 @@
             packed[pl.ds(filled, room), :] = rows[pl.ds(src * per + first, room), :]
             return filled + starts[src, slab + 1] - first
 
-        filled = lax.fori_loop(0, n_src, pack, jnp.int32(0))
-
-        @pl.loop(0, (filled + CHUNK - 1) // CHUNK)
-        def _(chunk):
-            base = pl.multiple_of(chunk * CHUNK, CHUNK)
-            f = packed[pl.ds(base, CHUNK), :].T[0:8]
+        filled = lax.fori_loop(0, n_src, pack, jnp.int32(0), unroll=4)
+
+        @pl.loop(0, (filled + GROUP - 1) // GROUP)
+        def _(group):
+            base = pl.multiple_of(group * GROUP, GROUP)
+            f = packed[pl.ds(base, GROUP), :].T[0:32]
             f = jnp.where(lanes + base < filled, f, 0.0)
             whole = f[0:3].astype(jnp.int32)
-            depth = whole[0:1] - slab * PLANES
             high_y, high_x = whole[1:2] // LOW, whole[2:3] // LOW
-            low_y, low_x = whole[1:2] - high_y * LOW, whole[2:3] - high_x * LOW
-            weight_z = placed(tap_weights(f[3:4], taps), depth, 2 * PLANES)
-            place_y = placed(tap_weights(f[4:5], taps), low_y, 2 * LOW)
-            place_x = placed(tap_weights(f[5:6], taps), low_x, 2 * LOW)
-            counter = lax.broadcasted_iota(jnp.int32, (NY // LOW, CHUNK), 0)
+            weight_z = placed(f[8:16], whole[0:1] - slab * PLANES, 2 * PLANES)
+            place_y = placed(f[16:24], whole[1:2] - high_y * LOW, 2 * LOW)
+            place_x = placed(f[24:32], whole[2:3] - high_x * LOW, 2 * LOW)
             hit_y = counter == high_y
-            hit_x = (counter == high_x).astype(F32)
+            hit_x = (counter == high_x).astype(F32).astype(BF16)
             value_y = jnp.concatenate([jnp.where(hit_y, f[6:7], 0.0), jnp.where(hit_y, f[7:8], 0.0)], axis=0)
             near, far = fine_dot(ty, place_y), fine_dot(hy, value_y)
             b_re = near[:ny] * far[:ny] - near[ny:] * far[ny:]
             b_im = near[:ny] * far[ny:] + near[ny:] * far[:ny]
-            near, far = fine_dot(tx, place_x), fine_dot(hx, hit_x)
+            near = fine_dot(tx, place_x)
+            far = jnp.dot(hx, jnp.concatenate([hit_x, hit_x], axis=0), preferred_element_type=F32)
             c_re = near[:nx] * far[:nx] - near[nx:] * far[nx:]
             c_im = near[:nx] * far[nx:] + near[nx:] * far[:nx]
-            right = jnp.concatenate(
-                [jnp.concatenate([c_re, -c_im], axis=1), jnp.concatenate([c_im, c_re], axis=1)], axis=0
-            )
-            right_high, right_low = halves(right)
-            both = jnp.concatenate([b_re, b_im], axis=1)
+            re_high, re_low = halves(c_re)
+            im_high, im_low = halves(c_im)
+            for part in range(GROUP // CHUNK):
+                cut = slice(part * CHUNK, (part + 1) * CHUNK)
+                chunk = group * (GROUP // CHUNK) + part
+                depths[chunk] = weight_z[:, cut]
+                both[chunk, :, :CHUNK] = b_re[:, cut]
+                both[chunk, :, CHUNK:] = b_im[:, cut]
+                for at, (re, im) in enumerate(((re_high, im_high), (re_high, im_high), (re_low, im_low))):
+                    first, second = at * 2 * CHUNK, (at * 2 + 1) * CHUNK
+                    right[chunk, :nx, first : first + CHUNK] = re[:, cut]
+                    right[chunk, :nx, second : second + CHUNK] = -im[:, cut]
+                    right[chunk, nx:, first : first + CHUNK] = im[:, cut]
+                    right[chunk, nx:, second : second + CHUNK] = re[:, cut]
+
+        @pl.loop(0, (filled + CHUNK - 1) // CHUNK)
+        def _(chunk):
             for z in range(WINDOW):
-                line = weight_z[z : z + 1]
-                high, low = halves(both * jnp.concatenate([line, line], axis=1))
+                line = depths[chunk, z : z + 1, :]
+                high, low = halves(both[chunk] * jnp.concatenate([line, line], axis=1))
                 left[z * ny : (z + 1) * ny, 0 : 2 * CHUNK] = high
                 left[z * ny : (z + 1) * ny, 2 * CHUNK : 4 * CHUNK] = low
                 left[z * ny : (z + 1) * ny, 4 * CHUNK : 6 * CHUNK] = high
-            right_all = jnp.concatenate([right_high, right_high, right_low], axis=1)
             sums = lax.dot_general(
-                left[...], right_all, (((1,), (1,)), ((), ())), preferred_element_type=F32
+                left[...], right[chunk], (((1,), (1,)), ((), ())), preferred_element_type=F32
             )
             at = pl.ds(pl.multiple_of(slab * (PLANES * ny), PLANES * ny), WINDOW * ny)
             grid_re[at, :] += sums[:, :nx]
             grid_im[at, :] += sums[:, nx:]
 
-    depth_all = table_z.shape[1]
-    tz = halves(table_z[...])
-
-    @pl.loop(0, ny)
+    tz = table_z[...]
+    depth_all = table_z.shape[1] // 3
+
+    @pl.loop(0, ny, unroll=4)
     def _(row):
         pick = pl.ds(row, depth_all, stride=ny)
         sums = fine_dot(tz, jnp.concatenate([grid_re[pick, :], grid_im[pick, :]], axis=1))
@@ -166,9 +245,11 @@
     tap_x = np.concatenate([cx, sx], axis=1)
     cx, sx = stacked(n_pencil, nx, far, NX)
     phase_x = np.concatenate([cx, sx], axis=1)
-    cz, sz = turns(np.arange(nz)[:, None], np.arange(nz + PLANES)[None, :], nz)
+    cz, sz = turns(np.arange(nz)[:, None], np.arange(nz + 2 * PLANES)[None, :], nz)
     table_z = np.concatenate([cz, sz], axis=0) / math.sqrt(nz * NY * NX)
-    return [x.astype(np.float32) for x in (tap_y, phase_y, tap_x, phase_x, table_z)]
+    stacks = [stack_left(x.astype(np.float32)) for x in (tap_y, phase_y, tap_x, table_z)]
+    exact_right = np.delete(stack_left(phase_x.astype(np.float32)), np.s_[: NY // LOW], axis=-1)
+    return stacks[0], stacks[1], stacks[2], exact_right, stacks[3]
 
 
 def shards(n_slab, n_pencil, sample_tile, sample_cell, sample_frac, sample_value):
@@ -188,11 +269,12 @@
     rank = jnp.sum((key[None, :] < key[:, None]).astype(jnp.int32), axis=1)
     shuffle = (rank[:, None] == order[None, :]).astype(F32)
     mine = jnp.dot(mine, shuffle, precision=lax.Precision.HIGHEST, preferred_element_type=F32)
-    feats = lax.all_gather(mine, ("slab", "pencil"), axis=0, tiled=False)
+    feats = gather_all(n_slab, n_pencil, mine)
     slab_of = feats[:, 0, :].astype(jnp.int32) // PLANES
     bins = jnp.arange(n_slab + 1, dtype=jnp.int32)
     starts = jnp.sum((slab_of[:, None, :] < bins[None, :, None]).astype(jnp.int32), axis=2)
     most = n_src * room
+    chunks = -(-most // GROUP) * (GROUP // CHUNK)
     vmem = pl.BlockSpec(memory_space=pltpu.VMEM)
     volume = pl.pallas_call(
         functools.partial(kernel, n_src, n_slab, per, room, ny, nz),
@@ -201,12 +283,15 @@
         out_specs=vmem,
         scratch_shapes=[
             pltpu.VMEM((n_src * per + room, 128), F32),
-            pltpu.VMEM((most + room, 128), F32),
-            pltpu.VMEM(((nz + PLANES) * ny, nx), F32),
-            pltpu.VMEM(((nz + PLANES) * ny, nx), F32),
+            pltpu.VMEM((-(-most // GROUP) * GROUP + room, 128), F32),
+            pltpu.VMEM(((nz + 2 * PLANES) * ny, nx), F32),
+            pltpu.VMEM(((nz + 2 * PLANES) * ny, nx), F32),
             pltpu.VMEM((WINDOW * ny, 6 * CHUNK), BF16),
+            pltpu.VMEM((chunks, ny, 2 * CHUNK), F32),
+            pltpu.VMEM((chunks, 2 * nx, 6 * CHUNK), BF16),
+            pltpu.VMEM((chunks, 2 * PLANES, CHUNK), F32),
         ],
-        compiler_params=pltpu.CompilerParams(vmem_limit_bytes=62 * 1024 * 1024),
+        compiler_params=pltpu.CompilerParams(vmem_limit_bytes=67043328),
         name="volume",
     )(starts, feats, *tables(n_slab, n_pencil, nz))
     return volume.reshape(2, nz, ny, nx)

time: 150 us -> 93.2 us (0.62); the launches traced: 148 us -> 93.7 us
  blocking collectives: 44 us -> 0 us
  Pallas kernels: 101 us -> 88.3 us
    all_gather x1 -> x0, blocking collectives: 44 us -> none  [shards(): feats = lax.all_gather(mine, ('slab', 'pencil'), axis=0, tiled=False)]
    pallas_call x1, Pallas kernels: 101 us -> 74.4 us  [shards(): pl.pallas_call(functools.partial(kernel, n_src, n_slab, per, room, ny, nz...]
    pallas_call x0 -> x1, Pallas kernels: none -> 13.9 us  [gather_all(): pl.pallas_call(functools.partial(gather_kernel, n_slab, n_pencil), out_sh...]
where the time goes in v2:
time: 93.2 us; the launch traced here: 93.7 us
  Pallas kernels  88.3 us (95%)
  other arithmetic  3.08 us (3%)
  matrix products  1.57 us (2%)
    pallas_call x1, Pallas kernels, shards(): pl.pallas_call(functools.partial(kernel, n_src, n_slab, per, room, ny, nz...  74.4 us
    pallas_call x1, Pallas kernels, gather_all(): pl.pallas_call(functools.partial(gather_kernel, n_slab, n_pencil), out_sh...  13.9 us

profile of v2, /device:TPU:0, one launch (start us, length us, event | category | flops | bytes accessed | tf_op | source)
XLA Modules:
  0.0 93.7 jit_solution(14585077701832783483)
XLA Ops:
  0.0 0.7 fusion.10
  0.7 0.8 iota_add_fusion
  1.5 0.2 convert_reduce_fusion.1
  1.7 1.6 %fusion.mine = f32[8,256]{1,0:T(8,128)} fusion(s32[256]{0:T(256)S(1)} %convert_reduce_fusion.1, f32[2,256]{1,0:T(2,128)} %param.12, f32[3,256]{1,0:T(4,128)} %param.11, f32[3,256]{1,0:T(4,128)S(1)} %add_convert_fusion), kind=kOutput, calls=%fused_computation.4 | convolution fusion | flops 6361088 | bytes 17408 | tf_op jit(solution)/shard_map/dot_general | solution.py:271
  3.3 13.9 %gather_samples.1.feats = f32[32,8,256]{2,1,0:T(8,128)} custom-call(f32[8,256]{1,0:T(8,128)} %fusion.mine), custom_call_target="tpu_custom_call" | custom-call | tf_op jit(solution)/shard_map/gather_samples/pallas_call | solution.py:116
  17.2 1.1 %and_select_fusion = s32[32,1,256]{2,1,0:T(1,128)S(1)} fusion(f32[32,8,256]{2,1,0:T(8,128)} %gather_samples.1.feats), kind=kLoop, calls=%fused_computation.6 | loop fusion | flops 131072 | bytes 65536 | tf_op jit(solution)/shard_map/jit(floor_divide)/jit(_where)/select_n | solution.py:273
  18.4 0.2 convert_reduce_fusion
  18.6 0.7 copy.10.starts
  19.3 74.4 %volume.1 = f32[2,4096,128]{2,1,0:T(8,128)} custom-call(s32[32,9]{1,0:T(8,128)} %copy.10.starts, f32[32,8,256]{2,1,0:T(8,128)} %gather_samples.1.feats, bf16[8,128,96]{2,1,0:T(8,128)(2,1)} %constant.57.clone.tap_y, bf16[8,128,192]{2,1,0:T(8,128)(2,1)} %constant.58.clone.phase_y, bf16[4,256,96]{2,1,0:T(8,128)(2,1)} %constant.59.clone.tap_x, ...), custom_call_target="tpu_custom_call" | custom-call | tf_op jit(solution)/shard_map/volume/pallas_call | solution.py:279
  (2 shorter events, 0.0 us)

commit v3 on v2

--- a/solution.py
+++ b/solution.py
@@ -17,6 +17,7 @@
 LOW = 16
 CHUNK = 128
 GROUP = 256
+BINS = 4
 BETA = 18.64
 F32 = jnp.float32
 BF16 = jnp.bfloat16
@@ -135,7 +136,8 @@
 ):
     slab_here = lax.axis_index("slab")
     pencil_here = lax.axis_index("pencil")
-    nx = out.shape[2]
+    nx = out.shape[3]
+    short = min(room, 16)
     taps = lax.broadcasted_iota(jnp.int32, (TAPS, per), 0).astype(F32)
 
     @pl.loop(0, n_src, unroll=2)
@@ -153,12 +155,25 @@
 
     @pl.loop(0, n_slab)
     def _(slab):
-        def pack(src, filled):
-            first = starts[src, slab]
-            packed[pl.ds(filled, room), :] = rows[pl.ds(src * per + first, room), :]
-            return filled + starts[src, slab + 1] - first
-
-        filled = lax.fori_loop(0, n_src, pack, jnp.int32(0), unroll=4)
+        ends = []
+        filled = jnp.int32(0)
+        for part in range(BINS):
+
+            def pack(src, filled, part=part):
+                first = starts[src, slab * BINS + part]
+                count = starts[src, slab * BINS + part + 1] - first
+                packed[pl.ds(filled, short), :] = rows[pl.ds(src * per + first, short), :]
+                if short < room:
+
+                    @pl.when(count > short)
+                    def _():
+                        rest = room - short
+                        packed[pl.ds(filled + short, rest), :] = rows[pl.ds(src * per + first + short, rest), :]
+
+                return filled + count
+
+            filled = lax.fori_loop(0, n_src, pack, filled, unroll=4)
+            ends.append(filled)
 
         @pl.loop(0, (filled + GROUP - 1) // GROUP)
         def _(group):
@@ -188,7 +203,7 @@
                 depths[chunk] = weight_z[:, cut]
                 both[chunk, :, :CHUNK] = b_re[:, cut]
                 both[chunk, :, CHUNK:] = b_im[:, cut]
-                for at, (re, im) in enumerate(((re_high, im_high), (re_high, im_high), (re_low, im_low))):
+                for at, (re, im) in enumerate(((re_high, im_high), (re_low, im_low))):
                     first, second = at * 2 * CHUNK, (at * 2 + 1) * CHUNK
                     right[chunk, :nx, first : first + CHUNK] = re[:, cut]
                     right[chunk, :nx, second : second + CHUNK] = -im[:, cut]
@@ -197,29 +212,48 @@
 
         @pl.loop(0, (filled + CHUNK - 1) // CHUNK)
         def _(chunk):
-            for z in range(WINDOW):
-                line = depths[chunk, z : z + 1, :]
-                high, low = halves(both[chunk] * jnp.concatenate([line, line], axis=1))
-                left[z * ny : (z + 1) * ny, 0 : 2 * CHUNK] = high
-                left[z * ny : (z + 1) * ny, 2 * CHUNK : 4 * CHUNK] = low
-                left[z * ny : (z + 1) * ny, 4 * CHUNK : 6 * CHUNK] = high
-            sums = lax.dot_general(
-                left[...], right[chunk], (((1,), (1,)), ((), ())), preferred_element_type=F32
-            )
-            at = pl.ds(pl.multiple_of(slab * (PLANES * ny), PLANES * ny), WINDOW * ny)
-            grid_re[at, :] += sums[:, :nx]
-            grid_im[at, :] += sums[:, nx:]
+            begin = chunk * CHUNK
+            final = jnp.minimum(begin + CHUNK, filled)
+            first = sum((end <= begin).astype(jnp.int32) for end in ends[:-1])
+            last = sum((end < final).astype(jnp.int32) for end in ends[:-1])
+            low_plane = first * (PLANES // BINS)
+            for span in range(BINS):
+
+                @pl.when(last - first == span)
+                def _(planes=(span + 1) * (PLANES // BINS) + TAPS - 1):
+                    here = both[chunk]
+                    for z in range(planes):
+                        line = depths[chunk, pl.ds(low_plane + z, 1), :]
+                        high, low = halves(here * jnp.concatenate([line, line], axis=1))
+                        left[z * ny : (z + 1) * ny, : 2 * CHUNK] = high
+                        left[z * ny : (z + 1) * ny, 2 * CHUNK :] = low
+                    high, low = left[: planes * ny, : 2 * CHUNK], left[: planes * ny, 2 * CHUNK :]
+                    right_high, right_low = right[chunk, :, : 2 * CHUNK], right[chunk, :, 2 * CHUNK :]
+                    sums = lax.dot_general(
+                        jnp.concatenate([high, low, high], axis=1),
+                        jnp.concatenate([right_high, right_high, right_low], axis=1),
+                        (((1,), (1,)), ((), ())),
+                        preferred_element_type=F32,
+                    )
+                    at = pl.ds(pl.multiple_of((slab * PLANES + low_plane) * ny, ny), planes * ny)
+                    grid_re[at, :] += sums[:, :nx]
+                    grid_im[at, :] += sums[:, nx:]
 
     tz = table_z[...]
     depth_all = table_z.shape[1] // 3
 
-    @pl.loop(0, ny, unroll=4)
-    def _(row):
-        pick = pl.ds(row, depth_all, stride=ny)
-        sums = fine_dot(tz, jnp.concatenate([grid_re[pick, :], grid_im[pick, :]], axis=1))
-        place = pl.ds(row, nz, stride=ny)
-        out[0, place, :] = sums[:nz, :nx] - sums[nz:, nx:]
-        out[1, place, :] = sums[nz:, :nx] + sums[:nz, nx:]
+    @pl.loop(0, ny // 8)
+    def _(block):
+        at = pl.ds(pl.multiple_of(block * 8, 8), 8)
+        g_re = jnp.swapaxes(grid_re.reshape(depth_all, ny, nx)[:, at, :], 0, 1)
+        g_im = jnp.swapaxes(grid_im.reshape(depth_all, ny, nx)[:, at, :], 0, 1)
+        done_re, done_im = [], []
+        for row in range(8):
+            sums = fine_dot(tz, jnp.concatenate([g_re[row], g_im[row]], axis=1))
+            done_re.append(sums[:nz, :nx] - sums[nz:, nx:])
+            done_im.append(sums[nz:, :nx] + sums[:nz, nx:])
+        out[0, :, at, :] = jnp.swapaxes(jnp.stack(done_re), 0, 1)
+        out[1, :, at, :] = jnp.swapaxes(jnp.stack(done_im), 0, 1)
 
 
 def turns(outer, inner, length):
@@ -270,15 +304,14 @@
     shuffle = (rank[:, None] == order[None, :]).astype(F32)
     mine = jnp.dot(mine, shuffle, precision=lax.Precision.HIGHEST, preferred_element_type=F32)
     feats = gather_all(n_slab, n_pencil, mine)
-    slab_of = feats[:, 0, :].astype(jnp.int32) // PLANES
-    bins = jnp.arange(n_slab + 1, dtype=jnp.int32)
-    starts = jnp.sum((slab_of[:, None, :] < bins[None, :, None]).astype(jnp.int32), axis=2)
+    bins = jnp.arange(n_slab * BINS + 1, dtype=jnp.int32) * (PLANES // BINS)
+    starts = jnp.sum((feats[:, 0, :].astype(jnp.int32)[:, None, :] < bins[None, :, None]).astype(jnp.int32), axis=2)
     most = n_src * room
     chunks = -(-most // GROUP) * (GROUP // CHUNK)
     vmem = pl.BlockSpec(memory_space=pltpu.VMEM)
     volume = pl.pallas_call(
         functools.partial(kernel, n_src, n_slab, per, room, ny, nz),
-        out_shape=jax.ShapeDtypeStruct((2, nz * ny, nx), F32),
+        out_shape=jax.ShapeDtypeStruct((2, nz, ny, nx), F32),
         in_specs=[pl.BlockSpec(memory_space=pltpu.SMEM)] + [vmem] * 6,
         out_specs=vmem,
         scratch_shapes=[
@@ -286,15 +319,15 @@
             pltpu.VMEM((-(-most // GROUP) * GROUP + room, 128), F32),
             pltpu.VMEM(((nz + 2 * PLANES) * ny, nx), F32),
             pltpu.VMEM(((nz + 2 * PLANES) * ny, nx), F32),
-            pltpu.VMEM((WINDOW * ny, 6 * CHUNK), BF16),
+            pltpu.VMEM((WINDOW * ny, 4 * CHUNK), BF16),
             pltpu.VMEM((chunks, ny, 2 * CHUNK), F32),
-            pltpu.VMEM((chunks, 2 * nx, 6 * CHUNK), BF16),
+            pltpu.VMEM((chunks, 2 * nx, 4 * CHUNK), BF16),
             pltpu.VMEM((chunks, 2 * PLANES, CHUNK), F32),
         ],
         compiler_params=pltpu.CompilerParams(vmem_limit_bytes=67043328),
         name="volume",
     )(starts, feats, *tables(n_slab, n_pencil, nz))
-    return volume.reshape(2, nz, ny, nx)
+    return volume
 
 
 def solution(mesh):

time: 93.2 us -> 93.5 us (level)
    select_n x1 -> x0, other arithmetic: 1.12 us -> none  [shards(): slab_of = feats[:, 0, :].astype(jnp.int32) // PLANES]
    convert_element_type x0 -> x1, other arithmetic: none -> 0.97 us  [shards(): feats[:, 0, :].astype(jnp.int32)[:, None, :] < bins[None, :, None]]
where the time goes in v3:
time: 93.5 us; the launch traced here: 93.4 us
  Pallas kernels  87.7 us (94%)
  other arithmetic  3.41 us (4%)
  matrix products  1.57 us (2%)
    pallas_call x1, Pallas kernels, shards(): pl.pallas_call(functools.partial(kernel, n_src, n_slab, per, room, ny, nz...  73.8 us
    pallas_call x1, Pallas kernels, gather_all(): pl.pallas_call(functools.partial(gather_kernel, n_slab, n_pencil), out_sh...  13.9 us

profile of v3, /device:TPU:0, one launch (start us, length us, event | category | flops | bytes accessed | tf_op | source)
XLA Modules:
  0.0 93.4 jit_solution(1640672052534799581)
XLA Ops:
  0.0 0.7 fusion.10
  0.7 0.8 iota_add_fusion
  1.5 0.2 convert_reduce_fusion.1
  1.7 1.6 %fusion.mine = f32[8,256]{1,0:T(8,128)} fusion(s32[256]{0:T(256)S(1)} %convert_reduce_fusion.1, f32[2,256]{1,0:T(2,128)} %param.12, f32[3,256]{1,0:T(4,128)} %param.11, f32[3,256]{1,0:T(4,128)S(1)} %add_convert_fusion), kind=kOutput, calls=%fused_computation.3 | convolution fusion | flops 6361088 | bytes 17408 | tf_op jit(solution)/shard_map/dot_general | solution.py:305
  3.3 13.9 %gather_samples.1.feats = f32[32,8,256]{2,1,0:T(8,128)} custom-call(f32[8,256]{1,0:T(8,128)} %fusion.mine), custom_call_target="tpu_custom_call" | custom-call | tf_op jit(solution)/shard_map/gather_samples/pallas_call | solution.py:117
  17.2 1.0 %slice_convert_fusion = s32[32,1,256]{2,1,0:T(1,128)S(1)} fusion(f32[32,8,256]{2,1,0:T(8,128)} %gather_samples.1.feats), kind=kLoop, calls=%fused_computation.6 | loop fusion | flops 8192 | bytes 65536 | tf_op jit(solution)/shard_map/convert_element_type | solution.py:308
  18.2 0.7 convert_reduce_fusion
  18.9 0.7 copy.10.starts
  19.6 73.8 %volume.1 = f32[2,64,64,128]{3,2,1,0:T(8,128)} custom-call(s32[32,33]{1,0:T(8,128)} %copy.10.starts, f32[32,8,256]{2,1,0:T(8,128)} %gather_samples.1.feats, bf16[8,128,96]{2,1,0:T(8,128)(2,1)} %constant.46.clone.tap_y, bf16[8,128,192]{2,1,0:T(8,128)(2,1)} %constant.47.clone.phase_y, bf16[4,256,96]{2,1,0:T(8,128)(2,1)} %constant.48.clone.tap_x, ...), custom_call_target="tpu_custom_call" | custom-call | tf_op jit(solution)/shard_map/volume/pallas_call | solution.py:312
  (3 shorter events, 0.0 us)

commit v4 on v3

--- a/solution.py
+++ b/solution.py
@@ -17,6 +17,7 @@
 LOW = 16
 CHUNK = 128
 GROUP = 256
+MAIN = 11
 BINS = 4
 BETA = 18.64
 F32 = jnp.float32
@@ -132,12 +133,12 @@
 def kernel(
     n_src, n_slab, per, room, ny, nz,
     starts, feats, tap_y, phase_y, tap_x, phase_x, table_z, out,
-    rows, packed, grid_re, grid_im, left, both, right, depths,
+    rows, packed, grid_re, grid_im, left_a, left_b, both, right, depths,
 ):
     slab_here = lax.axis_index("slab")
     pencil_here = lax.axis_index("pencil")
     nx = out.shape[3]
-    short = min(room, 16)
+    short = min(room, 24)
     taps = lax.broadcasted_iota(jnp.int32, (TAPS, per), 0).astype(F32)
 
     @pl.loop(0, n_src, unroll=2)
@@ -159,20 +160,26 @@
         filled = jnp.int32(0)
         for part in range(BINS):
 
-            def pack(src, filled, part=part):
-                first = starts[src, slab * BINS + part]
-                count = starts[src, slab * BINS + part + 1] - first
-                packed[pl.ds(filled, short), :] = rows[pl.ds(src * per + first, short), :]
-                if short < room:
-
-                    @pl.when(count > short)
-                    def _():
-                        rest = room - short
-                        packed[pl.ds(filled + short, rest), :] = rows[pl.ds(src * per + first + short, rest), :]
-
-                return filled + count
-
-            filled = lax.fori_loop(0, n_src, pack, filled, unroll=4)
+            def pack(quad, filled, part=part):
+                at = slab * BINS + part
+                picks = [(starts[quad * 4 + k, at], starts[quad * 4 + k, at + 1]) for k in range(4)]
+                places = [filled]
+                for first, end in picks:
+                    places.append(places[-1] + end - first)
+                longest = functools.reduce(jnp.maximum, [end - first for first, end in picks])
+
+                def move(size):
+                    for (first, _), place in zip(picks, places):
+                        packed[pl.ds(place, size), :] = rows[pl.ds(first, size), :]
+
+                if short == room:
+                    move(room)
+                else:
+                    pl.when(longest <= short)(functools.partial(move, short))
+                    pl.when(longest > short)(functools.partial(move, room))
+                return places[-1]
+
+            filled = lax.fori_loop(0, n_src // 4, pack, filled)
             ends.append(filled)
 
         @pl.loop(0, (filled + GROUP - 1) // GROUP)
@@ -182,7 +189,7 @@
             f = jnp.where(lanes + base < filled, f, 0.0)
             whole = f[0:3].astype(jnp.int32)
             high_y, high_x = whole[1:2] // LOW, whole[2:3] // LOW
-            weight_z = placed(f[8:16], whole[0:1] - slab * PLANES, 2 * PLANES)
+            weight_z = placed(f[8:16], whole[0:1] - slab * PLANES, 3 * PLANES)
             place_y = placed(f[16:24], whole[1:2] - high_y * LOW, 2 * LOW)
             place_x = placed(f[24:32], whole[2:3] - high_x * LOW, 2 * LOW)
             hit_y = counter == high_y
@@ -210,34 +217,53 @@
                     right[chunk, nx:, first : first + CHUNK] = im[:, cut]
                     right[chunk, nx:, second : second + CHUNK] = re[:, cut]
 
-        @pl.loop(0, (filled + CHUNK - 1) // CHUNK)
-        def _(chunk):
+        def bounds(chunk):
             begin = chunk * CHUNK
             final = jnp.minimum(begin + CHUNK, filled)
             first = sum((end <= begin).astype(jnp.int32) for end in ends[:-1])
             last = sum((end < final).astype(jnp.int32) for end in ends[:-1])
-            low_plane = first * (PLANES // BINS)
-            for span in range(BINS):
-
-                @pl.when(last - first == span)
-                def _(planes=(span + 1) * (PLANES // BINS) + TAPS - 1):
-                    here = both[chunk]
-                    for z in range(planes):
-                        line = depths[chunk, pl.ds(low_plane + z, 1), :]
-                        high, low = halves(here * jnp.concatenate([line, line], axis=1))
-                        left[z * ny : (z + 1) * ny, : 2 * CHUNK] = high
-                        left[z * ny : (z + 1) * ny, 2 * CHUNK :] = low
-                    high, low = left[: planes * ny, : 2 * CHUNK], left[: planes * ny, 2 * CHUNK :]
-                    right_high, right_low = right[chunk, :, : 2 * CHUNK], right[chunk, :, 2 * CHUNK :]
-                    sums = lax.dot_general(
-                        jnp.concatenate([high, low, high], axis=1),
-                        jnp.concatenate([right_high, right_high, right_low], axis=1),
-                        (((1,), (1,)), ((), ())),
-                        preferred_element_type=F32,
-                    )
-                    at = pl.ds(pl.multiple_of((slab * PLANES + low_plane) * ny, ny), planes * ny)
-                    grid_re[at, :] += sums[:, :nx]
-                    grid_im[at, :] += sums[:, nx:]
+            low_plane = jnp.minimum(first * (PLANES // BINS), WINDOW - MAIN)
+            return low_plane, (last + 1) * (PLANES // BINS) + TAPS - 1 > low_plane + MAIN
+
+        def form(left, chunk, low_plane, planes):
+            here = both[chunk]
+            for z in range(planes):
+                line = depths[chunk, pl.ds(low_plane + z, 1), :]
+                high, low = halves(here * jnp.concatenate([line, line], axis=1))
+                left[z * ny : (z + 1) * ny, : 2 * CHUNK] = high
+                left[z * ny : (z + 1) * ny, 2 * CHUNK :] = low
+
+        def multiply(left, chunk, low_plane, planes):
+            high, low = left[: planes * ny, : 2 * CHUNK], left[: planes * ny, 2 * CHUNK :]
+            right_high, right_low = right[chunk, :, : 2 * CHUNK], right[chunk, :, 2 * CHUNK :]
+            sums = lax.dot_general(
+                jnp.concatenate([high, low, high], axis=1),
+                jnp.concatenate([right_high, right_high, right_low], axis=1),
+                (((1,), (1,)), ((), ())),
+                preferred_element_type=F32,
+            )
+            at = pl.ds(pl.multiple_of((slab * PLANES + low_plane) * ny, ny), planes * ny)
+            grid_re[at, :] += sums[:, :nx]
+            grid_im[at, :] += sums[:, nx:]
+
+        form(left_a, 0, bounds(0)[0], MAIN)
+
+        @pl.loop(0, (filled + GROUP - 1) // GROUP)
+        def _(pair):
+            one, two = pair * 2, pair * 2 + 1
+            low_one, more_one = bounds(one)
+            low_two, more_two = bounds(two)
+            low_next, _ = bounds(two + 1)
+            multiply(left_a, one, low_one, MAIN)
+            form(left_b, two, low_two, MAIN)
+            multiply(left_b, two, low_two, MAIN)
+            form(left_a, two + 1, low_next, MAIN)
+            for chunk, low_plane, more in ((one, low_one, more_one), (two, low_two, more_two)):
+
+                @pl.when(more)
+                def _(chunk=chunk, low_plane=low_plane):
+                    form(left_b, chunk, low_plane + MAIN, WINDOW - MAIN)
+                    multiply(left_b, chunk, low_plane + MAIN, WINDOW - MAIN)
 
     tz = table_z[...]
     depth_all = table_z.shape[1] // 3
@@ -305,7 +331,9 @@
     mine = jnp.dot(mine, shuffle, precision=lax.Precision.HIGHEST, preferred_element_type=F32)
     feats = gather_all(n_slab, n_pencil, mine)
     bins = jnp.arange(n_slab * BINS + 1, dtype=jnp.int32) * (PLANES // BINS)
-    starts = jnp.sum((feats[:, 0, :].astype(jnp.int32)[:, None, :] < bins[None, :, None]).astype(jnp.int32), axis=2)
+    planes = feats[:, 0, :].astype(jnp.int32)
+    starts = jnp.sum((planes[:, None, :] < bins[None, :, None]).astype(jnp.int32), axis=2)
+    starts = starts + jnp.arange(n_src, dtype=jnp.int32)[:, None] * per
     most = n_src * room
     chunks = -(-most // GROUP) * (GROUP // CHUNK)
     vmem = pl.BlockSpec(memory_space=pltpu.VMEM)
@@ -319,10 +347,11 @@
             pltpu.VMEM((-(-most // GROUP) * GROUP + room, 128), F32),
             pltpu.VMEM(((nz + 2 * PLANES) * ny, nx), F32),
             pltpu.VMEM(((nz + 2 * PLANES) * ny, nx), F32),
-            pltpu.VMEM((WINDOW * ny, 4 * CHUNK), BF16),
-            pltpu.VMEM((chunks, ny, 2 * CHUNK), F32),
+            pltpu.VMEM((MAIN * ny, 4 * CHUNK), BF16),
+            pltpu.VMEM((MAIN * ny, 4 * CHUNK), BF16),
+            pltpu.VMEM((chunks + 1, ny, 2 * CHUNK), F32),
             pltpu.VMEM((chunks, 2 * nx, 4 * CHUNK), BF16),
-            pltpu.VMEM((chunks, 2 * PLANES, CHUNK), F32),
+            pltpu.VMEM((chunks + 1, 3 * PLANES, CHUNK), F32),
         ],
         compiler_params=pltpu.CompilerParams(vmem_limit_bytes=67043328),
         name="volume",

time: 93.5 us -> 89.1 us (0.953); the launches traced: 93.4 us -> 90 us
  Pallas kernels: 87.7 us -> 84.2 us
    pallas_call x1, Pallas kernels: 73.8 us -> 70.3 us  [shards(): pl.pallas_call(functools.partial(kernel, n_src, n_slab, per, room, ny, nz...]
where the time goes in v4:
time: 89.1 us; the launch traced here: 90 us
  Pallas kernels  84.2 us (95%)
  other arithmetic  4.09 us (5%)
  matrix products  1.57 us (2%)
    pallas_call x1, Pallas kernels, shards(): pl.pallas_call(functools.partial(kernel, n_src, n_slab, per, room, ny, nz...  70.3 us
    pallas_call x1, Pallas kernels, gather_all(): pl.pallas_call(functools.partial(gather_kernel, n_slab, n_pencil), out_sh...  13.9 us

profile of v4, /device:TPU:0, one launch (start us, length us, event | category | flops | bytes accessed | tf_op | source)
XLA Modules:
  0.0 90.0 jit_solution(17331075677144206739)
XLA Ops:
  0.0 0.7 fusion.10
  0.7 0.8 iota_add_fusion
  1.5 0.2 convert_reduce_fusion.1
  1.7 1.6 %fusion.mine = f32[8,256]{1,0:T(8,128)} fusion(s32[256]{0:T(256)S(1)} %convert_reduce_fusion.1, f32[2,256]{1,0:T(2,128)} %param.12, f32[3,256]{1,0:T(4,128)} %param.11, f32[3,256]{1,0:T(4,128)S(1)} %add_convert_fusion), kind=kOutput, calls=%fused_computation.3 | convolution fusion | flops 6361088 | bytes 17408 | tf_op jit(solution)/shard_map/dot_general | solution.py:331
  3.3 13.9 %gather_samples.1.feats = f32[32,8,256]{2,1,0:T(8,128)} custom-call(f32[8,256]{1,0:T(8,128)} %fusion.mine), custom_call_target="tpu_custom_call" | custom-call | tf_op jit(solution)/shard_map/gather_samples/pallas_call | solution.py:118
  17.2 1.0 %slice_convert_fusion = s32[32,1,256]{2,1,0:T(1,128)S(1)} fusion(f32[32,8,256]{2,1,0:T(8,128)} %gather_samples.1.feats), kind=kLoop, calls=%fused_computation.6 | loop fusion | flops 8192 | bytes 65536 | tf_op jit(solution)/shard_map/convert_element_type | solution.py:334
  18.2 0.7 convert_reduce_fusion
  18.9 0.1 copy.10
  19.0 0.7 broadcast_add_fusion.starts
  19.7 70.3 %volume.1 = f32[2,64,64,128]{3,2,1,0:T(8,128)} custom-call(s32[32,33]{1,0:T(8,128)} %broadcast_add_fusion.starts, f32[32,8,256]{2,1,0:T(8,128)} %gather_samples.1.feats, bf16[8,128,96]{2,1,0:T(8,128)(2,1)} %constant.47.clone.tap_y, bf16[8,128,192]{2,1,0:T(8,128)(2,1)} %constant.48.clone.phase_y, bf16[4,256,96]{2,1,0:T(8,128)(2,1)} %constant.49.clone.tap_x, ...), custom_call_target="tpu_custom_call" | custom-call | tf_op jit(solution)/shard_map/volume/pallas_call | solution.py:340
  (4 shorter events, 0.0 us)

commit v5 on v4

--- a/solution.py
+++ b/solution.py
@@ -69,32 +69,38 @@
     return jnp.dot(left, jnp.concatenate([high, low, high], axis=0), preferred_element_type=F32)
 
 
-def gather_kernel(n_slab, n_pencil, mine, out, send_sem, recv_sem, own_sem):
-    count = n_slab * n_pencil
-    me = lax.axis_index("slab") * n_pencil + lax.axis_index("pencil")
+def gather_kernel(n_slab, n_pencil, mine, out, send_sem, recv_sem, own_sem, pair_send, pair_recv):
+    half = n_pencil // 2
+    count = n_slab * half
+    slab, pencil = lax.axis_index("slab"), lax.axis_index("pencil")
+    parity = lax.rem(pencil, 2)
+    me = slab * half + pencil // 2
+    partner = {"slab": slab, "pencil": pencil + 1 - 2 * parity}
+    mesh_id = pl.DeviceIdType.MESH
 
     def name(step):
         target = lax.rem(me + step, count)
-        return {"slab": target // n_pencil, "pencil": lax.rem(target, n_pencil)}
-
-    own = pltpu.make_async_copy(mine, out.at[me], own_sem)
+        return {"slab": target // half, "pencil": lax.rem(target, half) * 2 + parity}
+
+    own = pltpu.make_async_copy(mine, out.at[parity * count + me], own_sem)
     own.start()
     barrier = pltpu.get_barrier_semaphore()
 
     @pl.loop(1, count)
     def _(step):
-        pl.semaphore_signal(barrier, inc=1, device_id=name(step), device_id_type=pl.DeviceIdType.MESH)
-
-    pl.semaphore_wait(barrier, count - 1)
+        pl.semaphore_signal(barrier, inc=1, device_id=name(step), device_id_type=mesh_id)
+
+    pl.semaphore_signal(barrier, inc=1, device_id=partner, device_id_type=mesh_id)
+    pl.semaphore_wait(barrier, count)
 
     def send(step, slot):
         return pltpu.make_async_remote_copy(
             src_ref=mine,
-            dst_ref=out.at[slot],
+            dst_ref=out.at[parity * count + slot],
             send_sem=send_sem.at[step - 1],
             recv_sem=recv_sem.at[step - 1],
             device_id=name(step),
-            device_id_type=pl.DeviceIdType.MESH,
+            device_id_type=mesh_id,
         )
 
     @pl.loop(1, count)
@@ -107,9 +113,17 @@
     def _(step):
         send(step, lax.rem(me + count - step, count)).wait_recv()
 
+    ours = out.at[pl.ds(parity * count, count)]
+    across = pltpu.make_async_remote_copy(
+        src_ref=ours, dst_ref=ours, send_sem=pair_send, recv_sem=pair_recv, device_id=partner, device_id_type=mesh_id
+    )
+    across.start()
+
     @pl.loop(1, count)
     def _(step):
         send(step, me).wait_send()
+
+    across.wait()
 
 
 def gather_all(n_slab, n_pencil, mine):
@@ -121,8 +135,10 @@
         in_specs=[vmem],
         out_specs=vmem,
         scratch_shapes=[
-            pltpu.SemaphoreType.DMA((count - 1,)),
-            pltpu.SemaphoreType.DMA((count - 1,)),
+            pltpu.SemaphoreType.DMA((count // 2 - 1,)),
+            pltpu.SemaphoreType.DMA((count // 2 - 1,)),
+            pltpu.SemaphoreType.DMA,
+            pltpu.SemaphoreType.DMA,
             pltpu.SemaphoreType.DMA,
         ],
         compiler_params=pltpu.CompilerParams(collective_id=0, has_side_effects=True),

time: 89.1 us -> 87.1 us (0.978)
  Pallas kernels: 84.2 us -> 81.6 us
    pallas_call x1, Pallas kernels: 70.3 us -> 69 us  [shards(): pl.pallas_call(functools.partial(kernel, n_src, n_slab, per, room, ny, nz...]
    pallas_call x1, Pallas kernels: 13.9 us -> 12.6 us  [gather_all(): pl.pallas_call(functools.partial(gather_kernel, n_slab, n_pencil), out_sh...]
where the time goes in v5:
time: 87.1 us; the launch traced here: 87.4 us
  Pallas kernels  81.6 us (94%)
  other arithmetic  4.09 us (5%)
  matrix products  1.57 us (2%)
    pallas_call x1, Pallas kernels, shards(): pl.pallas_call(functools.partial(kernel, n_src, n_slab, per, room, ny, nz...  69 us
    pallas_call x1, Pallas kernels, gather_all(): pl.pallas_call(functools.partial(gather_kernel, n_slab, n_pencil), out_sh...  12.6 us

profile of v5, /device:TPU:0, one launch (start us, length us, event | category | flops | bytes accessed | tf_op | source)
XLA Modules:
  0.0 87.4 jit_solution(16668578561461703972)
XLA Ops:
  0.0 0.7 fusion.10
  0.7 0.8 iota_add_fusion
  1.5 0.2 convert_reduce_fusion.1
  1.7 1.6 %fusion.mine = f32[8,256]{1,0:T(8,128)} fusion(s32[256]{0:T(256)S(1)} %convert_reduce_fusion.1, f32[2,256]{1,0:T(2,128)} %param.12, f32[3,256]{1,0:T(4,128)} %param.11, f32[3,256]{1,0:T(4,128)S(1)} %add_convert_fusion), kind=kOutput, calls=%fused_computation.3 | convolution fusion | flops 6361088 | bytes 17408 | tf_op jit(solution)/shard_map/dot_general | solution.py:347
  3.3 12.6 %gather_samples.1.feats = f32[32,8,256]{2,1,0:T(8,128)} custom-call(f32[8,256]{1,0:T(8,128)} %fusion.mine), custom_call_target="tpu_custom_call" | custom-call | tf_op jit(solution)/shard_map/gather_samples/pallas_call | solution.py:132
  15.9 1.0 %slice_convert_fusion = s32[32,1,256]{2,1,0:T(1,128)S(1)} fusion(f32[32,8,256]{2,1,0:T(8,128)} %gather_samples.1.feats), kind=kLoop, calls=%fused_computation.6 | loop fusion | flops 8192 | bytes 65536 | tf_op jit(solution)/shard_map/convert_element_type | solution.py:350
  16.9 0.7 convert_reduce_fusion
  17.6 0.1 copy.10
  17.7 0.7 broadcast_add_fusion.starts
  18.4 69.0 %volume.1 = f32[2,64,64,128]{3,2,1,0:T(8,128)} custom-call(s32[32,33]{1,0:T(8,128)} %broadcast_add_fusion.starts, f32[32,8,256]{2,1,0:T(8,128)} %gather_samples.1.feats, bf16[8,128,96]{2,1,0:T(8,128)(2,1)} %constant.47.clone.tap_y, bf16[8,128,192]{2,1,0:T(8,128)(2,1)} %constant.48.clone.phase_y, bf16[4,256,96]{2,1,0:T(8,128)(2,1)} %constant.49.clone.tap_x, ...), custom_call_target="tpu_custom_call" | custom-call | tf_op jit(solution)/shard_map/volume/pallas_call | solution.py:356
  (4 shorter events, 0.0 us)
